TPU v7x, 256 devices: a whole 4x4x8 slice. The times are simulated.
256 devices in a mesh: span: 32 (over z_hi, y, x_hi), cols: 2 (over z_lo), copy: 4 (over x_lo, core).
Axes of the slice: x: 4 (x_hi: 2, x_lo: 2; x = x_hi * 2 + x_lo), y: 4, z: 8 (z_hi: 4, z_lo: 2; z = z_hi * 2 + z_lo), core: 2. Of those that a mesh axis runs over, the one named last changes fastest.
Arguments:
- leak_rate: float32 [8, 4096, 2560], P('copy', 'span', 'cols'), parts along dimension 0, may hold values from 0.2 to 2
- signal_in: bfloat16 [8, 4096, 2560], P('copy', 'span', 'cols'), parts along dimension 0, may hold values from -6 to 6
- gate_in: bfloat16 [8, 4096, 2560], P('copy', 'span', 'cols'), parts along dimension 0, may hold values from -6 to 6
Outputs:
- sequence_out: bfloat16 [8, 4096, 2560], P('copy', 'span', 'cols'), parts along dimension 0
There are 4 independent parts, one for each index of `copy`. A program takes and returns all parts, laid end to end along the dimension named above; each array names one. Nothing has to cross between parts.
All inputs are finite; a program needn't handle non-finite values.
Results may differ from a plain program's by a relative error of at most 0.001.
Values sent between devices are 32-bit elements; how exact they have to be, the bound alone decides.
A program may use at most 64 MiB of HBM per device.

v0:
```python
import jax
import jax.numpy as jnp
from jax import lax
from jax.sharding import Mesh
from jax.sharding import PartitionSpec as P

SPAN = ("span_0", "span_1", "span_2")


def from_everyone(value, axis):
    peers = lax.axis_size(axis)
    return lax.all_to_all(
        jnp.broadcast_to(value[None], (peers, *value.shape)), axis, 0, 0, tiled=True
    )


def collected_together(value, axis):
    leaves = jax.tree.leaves(value)
    order = sorted(range(len(leaves)), key=lambda k: -leaves[k].size)
    width = (1, *leaves[order[0]].shape)[-1]
    lines = [
        jnp.pad(leaves[k].reshape(-1), (0, -leaves[k].size % width)).reshape(-1, width)
        for k in order
    ]
    both, at, found = (from_everyone(jnp.concatenate(lines), axis), 0, {})
    for k, line in zip(order, lines):
        share = both[:, at : at + len(line)].reshape(len(both), -1)
        found[k] = share[:, : leaves[k].size].reshape(-1, *leaves[k].shape)
        at += len(line)
    numbers = iter(range(len(leaves)))
    return jax.tree.map(lambda _: found[next(numbers)], value)


def combined_pairwise(pieces, combine):
    while len(jax.tree.leaves(pieces)[0]) > 1:
        pieces = jax.vmap(combine)(
            *(jax.tree.map(lambda part: part[side::2], pieces) for side in (0, 1))
        )
    return jax.tree.map(lambda part: part[0], pieces)


def carried_in(value, axis, combine, identity):
    peers, mine = (lax.axis_size(axis), lax.axis_index(axis))
    passed = jnp.arange(peers) < mine

    def kept(part, zero, own):
        part = jnp.where(
            passed.reshape(-1, *(1 for _ in own.shape)), part, jnp.asarray(zero, own.dtype)
        )
        return part

    pieces = collected_together(value, axis)
    return combined_pairwise(jax.tree.map(kept, pieces, identity, value), combine)


def filled_with(value, identity):
    return jax.tree.map(
        lambda a, e: jnp.broadcast_to(jnp.asarray(e, a.dtype), a.shape), value, identity
    )


def all_in_one(value, axis):
    leaves = jax.tree.leaves(value)
    order = sorted(range(len(leaves)), key=lambda k: -leaves[k].size)
    width = (1, *leaves[order[0]].shape)[-1]
    lines = [
        jnp.pad(leaves[k].reshape(-1), (0, -leaves[k].size % width)).reshape(-1, width)
        for k in order
    ]
    both, at, found = (lax.all_gather(jnp.concatenate(lines), axis), 0, {})
    for k, line in zip(order, lines):
        share = both[:, at : at + len(line)].reshape(len(both), -1)
        found[k] = share[:, : leaves[k].size].reshape(-1, *leaves[k].shape)
        at += len(line)
    numbers = iter(range(len(leaves)))
    return jax.tree.map(lambda _: found[next(numbers)], value)


def carried_in_2(value, axes, combine, identity):
    before = start = filled_with(value, identity)
    total = value
    for axis in reversed(axes):
        peers, mine = (lax.axis_size(axis), lax.axis_index(axis))
        pieces = all_in_one(total, axis)
        inside, total = (start, start)
        for k in reversed(range(peers)):
            passed = k > mine
            total = combine(total, jax.tree.map(lambda part: part[k], pieces))
            inside = jax.tree.map(lambda new, old: jnp.where(passed, new, old), total, inside)
        before = combine(inside, before)
    return before


def join_pair(earlier, later):
    return (earlier[0] * later[0], later[0] * earlier[1] + later[1])


def body(leak_rate, signal_in, gate_in):
    total_length = leak_rate.shape[1] * lax.axis_size(SPAN)
    keep = jnp.exp(-leak_rate / total_length)
    push = signal_in.astype(jnp.float32) * total_length ** (-0.5)
    product, forward = lax.associative_scan(join_pair, (keep, push), axis=1)
    entering_forward = carried_in(
        (product[:, -1], forward[:, -1]),
        SPAN,
        join_pair,
        (jnp.ones_like(keep[:, 0]), jnp.zeros_like(push[:, 0])),
    )
    forward = forward + product * entering_forward[1][:, None]
    product, backward = lax.associative_scan(join_pair, (keep, push), axis=1, reverse=True)
    entering_backward = carried_in_2(
        (product[:, 0], backward[:, 0]),
        SPAN,
        join_pair,
        (jnp.ones_like(keep[:, 0]), jnp.zeros_like(push[:, 0])),
    )
    backward = backward + product * entering_backward[1][:, None]
    states = forward + backward
    gated = states * jax.nn.silu(gate_in.astype(jnp.float32))
    sequence_out = gated.astype(jnp.bfloat16)
    return sequence_out


def solution(mesh):
    split = Mesh(
        mesh.devices.reshape(4, 4, 2, mesh.shape["cols"], mesh.shape["copy"]),
        ("span_0", "span_1", "span_2", "cols", "copy"),
    )
    placed = (P("copy", SPAN, "cols"), P("copy", SPAN, "cols"), P("copy", SPAN, "cols"))
    return jax.shard_map(
        body, mesh=split, in_specs=placed, out_specs=P("copy", SPAN, "cols"), check_vma=False
    )
```

profile of v0, /device:TPU:2, one launch (start us, length us, event | category | flops | bytes accessed | tf_op | source)
XLA Modules:
  0.0 162.4 jit_solution(6295568818081287394)
XLA Ops:
  2.1 2.3 %slice.574 = f32[2,64,1280]{2,1,0:T(8,128)} slice(f32[2,128,1280]{2,1,0:T(8,128)S(1)} %multiply_exponential_fusion), slice={[0:2:1], [1:128:2], [0:1280:1]} | slice | bytes 1310720 | tf_op jit(solution)/shard_map/slice | solution.py:102
  4.4 2.2 %slice.573 = f32[2,63,1280]{2,1,0:T(8,128)} slice(f32[2,128,1280]{2,1,0:T(8,128)S(1)} %multiply_exponential_fusion), slice={[0:2:1], [2:128:2], [0:1280:1]} | slice | bytes 1290240 | tf_op jit(solution)/shard_map/slice | solution.py:102
  7.8 2.3 %slice.622 = f32[2,63,1280]{2,1,0:T(8,128)} slice(f32[2,128,1280]{2,1,0:T(8,128)S(1)} %broadcast_multiply_fusion.1), slice={[0:2:1], [2:128:2], [0:1280:1]} | slice | bytes 1290240 | tf_op jit(solution)/shard_map/slice | solution.py:102
  10.1 2.1 %slice.576 = f32[2,64,1280]{2,1,0:T(8,128)} slice(f32[2,128,1280]{2,1,0:T(8,128)S(1)} %broadcast_multiply_fusion.1), slice={[0:2:1], [1:128:2], [0:1280:1]} | slice | bytes 1310720 | tf_op jit(solution)/shard_map/slice | solution.py:102
  12.2 2.2 %slice.575 = f32[2,64,1280]{2,1,0:T(8,128)} slice(f32[2,128,1280]{2,1,0:T(8,128)S(1)} %broadcast_multiply_fusion.1), slice={[0:2:1], [0:127:2], [0:1280:1]} | slice | bytes 1310720 | tf_op jit(solution)/shard_map/slice | solution.py:102
  29.1 2.7 %pad.197 = f32[2,64,1280]{2,1,0:T(8,128)} pad(f32[2,32,1280]{2,1,0:T(8,128)} %add.420, f32[]{:T(128)} %constant.15.clone.1), padding=0_0_0x1_0_1x0_0_0 | pad | bytes 983044 | tf_op jit(solution)/shard_map/pad | solution.py:102
  31.8 2.0 %add.421 = f32[2,64,1280]{2,1,0:T(8,128)} add(f32[2,64,1280]{2,1,0:T(8,128)S(1)} %pad.196, f32[2,64,1280]{2,1,0:T(8,128)} %pad.197) | non-fusion elementwise | flops 163840 | bytes 1966080 | tf_op jit(solution)/shard_map/add | solution.py:102
  39.9 3.2 %pad.184 = f32[2,128,1280]{2,1,0:T(8,128)} pad(f32[2,64,1280]{2,1,0:T(8,128)} %pad_maximum_fusion, f32[]{:T(128)} %constant.15.clone.1), padding=0_0_0x0_1_1x0_0_0 | pad | bytes 1966084 | tf_op jit(solution)/shard_map/pad | solution.py:102
  43.1 3.2 %pad.185 = f32[2,128,1280]{2,1,0:T(8,128)} pad(f32[2,64,1280]{2,1,0:T(8,128)} %add.413, f32[]{:T(128)} %constant.15.clone.1), padding=0_0_0x1_0_1x0_0_0 | pad | bytes 1966084 | tf_op jit(solution)/shard_map/pad | solution.py:102
  47.2 2.3 %pad.199 = f32[2,128,1280]{2,1,0:T(8,128)} pad(f32[2,64,1280]{2,1,0:T(8,128)S(1)} %copy-done.14, f32[]{:T(128)} %constant.15.clone.1), padding=0_0_0x1_0_1x0_0_0 | pad | bytes 1966084 | tf_op jit(solution)/shard_map/pad | solution.py:102
  51.5 13.5 %all-to-all-start = ((f32[32,4,1280]{2,1,0:T(4,128)}), f32[32,4,1280]{2,1,0:T(4,128)}, u32[]{:S(2)}, u32[]{:S(2)}) async-start(f32[32,4,1280]{2,1,0:T(4,128)} %broadcast_in_dim.26), calls=%async_computation | async-start | bytes 1310720 | tf_op jit(solution)/shard_map/all_to_all | solution.py:12
  65.0 3.2 %slice.666 = f32[2,64,1280]{2,1,0:T(8,128)} reverse(f32[2,64,1280]{2,1,0:T(8,128)S(1)} %copy-done.3), dimensions={1} | reverse | bytes 1310720 | tf_op jit(solution)/shard_map/slice | solution.py:110
  68.2 3.3 %slice.662 = f32[2,64,1280]{2,1,0:T(8,128)} reverse(f32[2,64,1280]{2,1,0:T(8,128)S(1)} %copy-done.2), dimensions={1} | reverse | bytes 1310720 | tf_op jit(solution)/shard_map/slice | solution.py:110
  72.1 7.8 %reverse.9 = f32[2,128,1280]{2,1,0:T(8,128)S(1)} reverse(bf16[2,128,1280]{2,1,0:T(8,128)(2,1)} %param.4), dimensions={1} | reverse | bytes 1966080 | tf_op jit(solution)/shard_map/reverse
  80.1 2.3 %slice.710 = f32[2,63,1280]{2,1,0:T(8,128)} slice(f32[2,128,1280]{2,1,0:T(8,128)S(1)} %broadcast_multiply_fusion), slice={[0:2:1], [2:128:2], [0:1280:1]} | slice | bytes 1290240 | tf_op jit(solution)/shard_map/slice | solution.py:110
  82.3 2.2 %slice.664 = f32[2,64,1280]{2,1,0:T(8,128)} slice(f32[2,128,1280]{2,1,0:T(8,128)S(1)} %broadcast_multiply_fusion), slice={[0:2:1], [1:128:2], [0:1280:1]} | slice | bytes 1310720 | tf_op jit(solution)/shard_map/slice | solution.py:110
  84.5 2.2 %slice.663 = f32[2,64,1280]{2,1,0:T(8,128)} slice(f32[2,128,1280]{2,1,0:T(8,128)S(1)} %broadcast_multiply_fusion), slice={[0:2:1], [0:127:2], [0:1280:1]} | slice | bytes 1310720 | tf_op jit(solution)/shard_map/slice | solution.py:110
  90.8 3.3 %slice.661 = f32[2,63,1280]{2,1,0:T(8,128)} reverse(f32[2,63,1280]{2,1,0:T(8,128)S(1)} %slice.660), dimensions={1} | reverse | bytes 1290240 | tf_op jit(solution)/shard_map/slice | solution.py:110
  104.8 10.9 %rev.12 = f32[2,128,1280]{2,1,0:T(8,128)} reverse(f32[2,128,1280]{2,1,0:T(8,128)} %add.457), dimensions={1} | reverse | bytes 2621440 | tf_op jit(solution)/shard_map/rev | solution.py:110
  115.7 6.5 %rev.11 = f32[2,128,1280]{2,1,0:T(8,128)} reverse(f32[2,128,1280]{2,1,0:T(8,128)S(1)} %copy-done.7), dimensions={1} | reverse | bytes 2621440 | tf_op jit(solution)/shard_map/rev | solution.py:110
  122.2 6.0 %all-gather.3 = f32[2,4,1280]{2,1,0:T(4,128)S(1)} all-gather(f32[1,4,1280]{2,1,0:T(4,128)S(1)} %maximum_bitcast_fusion), channel_id=2, replica_groups=mesh['span_0'=4,'span_1'=4,'span_2'=2,'cols'=2,'copy'=4] {'span_2'}, dimensions={0}, use_global_device_ids=true | all-gather | bytes 61440 | tf_op jit(solution)/shard_map/all_gather | solution.py:70
  128.2 12.3 %all-gather.4 = f32[4,4,1280]{2,1,0:T(4,128)S(1)} all-gather(f32[1,4,1280]{2,1,0:T(4,128)S(1)} %maximum_bitcast_fusion.1), channel_id=3, replica_groups=mesh['span_0'=4,'span_1'=4,'span_2'=2,'cols'=2,'copy'=4] {'span_1'}, dimensions={0}, use_global_device_ids=true | all-gather | bytes 102400 | tf_op jit(solution)/shard_map/all_gather | solution.py:70
  140.6 15.5 %all-gather.5 = f32[4,4,1280]{2,1,0:T(4,128)S(1)} all-gather(f32[1,4,1280]{2,1,0:T(4,128)S(1)} %maximum_bitcast_fusion.2), channel_id=4, replica_groups=mesh['span_0'=4,'span_1'=4,'span_2'=2,'cols'=2,'copy'=4] {'span_0'}, dimensions={0}, use_global_device_ids=true | all-gather | bytes 102400 | tf_op jit(solution)/shard_map/all_gather | solution.py:70
  158.4 4.0 %fusion.4 = bf16[2,128,1280]{2,1,0:T(8,128)(2,1)} fusion(bf16[2,128,1280]{2,1,0:T(8,128)(2,1)S(1)} %copy-done.20, f32[2,128,1280]{2,1,0:T(8,128)} %rev.11, f32[2,128,1280]{2,1,0:T(8,128)} %rev.12, f32[2,128,1280]{2,1,0:T(8,128)S(1)} %copy-done.5, f32[2,128,1280]{2,1,0:T(8,128)} %pad.199, f32[2,128,1280]{2,1,0:T(8,128)S(1)} %copy-done.6, ...), kind=kLoop, calls=%fused_computation.7 | loop fusion | flops 4587520 | bytes 9195520 | tf_op jit(solution)/shard_map/convert_element_type | solution.py:120
  (261 shorter events, 43.7 us)
Async XLA Ops:
  2.1 12.3 %copy-start.1 = (f32[2,64,1280]{2,1,0:T(8,128)}, f32[2,64,1280]{2,1,0:T(8,128)S(1)}, u32[]{:S(2)}) copy-start(f32[2,64,1280]{2,1,0:T(8,128)S(1)} %slice.578) | copy-start | bytes 1966084
  18.6 1.9 %copy-start.19 = (f32[2,32,1280]{2,1,0:T(8,128)S(1)}, f32[2,32,1280]{2,1,0:T(8,128)}, u32[]{:S(2)}) copy-start(f32[2,32,1280]{2,1,0:T(8,128)} %slice.582) | copy-start | bytes 983044
  24.4 1.6 copy-start.17
  26.8 1.0 copy-start.18
  33.8 1.3 copy-start
  33.8 1.5 copy-start.10
  33.8 1.7 %copy-start.11 = (f32[2,63,1280]{2,1,0:T(8,128)S(1)}, f32[2,63,1280]{2,1,0:T(8,128)}, u32[]{:S(2)}) copy-start(f32[2,63,1280]{2,1,0:T(8,128)} %slice.622) | copy-start | bytes 1935364
  37.5 1.3 copy-start.8
  38.9 10.7 %copy-start.4 = (f32[2,128,1280]{2,1,0:T(8,128)}, f32[2,128,1280]{2,1,0:T(8,128)S(1)}, u32[]{:S(2)}) copy-start(f32[2,128,1280]{2,1,0:T(8,128)S(1)} %pad.198) | copy-start | bytes 3932164
  43.1 4.2 %copy-start.14 = (f32[2,64,1280]{2,1,0:T(8,128)S(1)}, f32[2,64,1280]{2,1,0:T(8,128)}, u32[]{:S(2)}) copy-start(f32[2,64,1280]{2,1,0:T(8,128)} %add.421) | copy-start | bytes 1966084
  49.5 15.5 %copy-start.3 = (f32[2,64,1280]{2,1,0:T(8,128)S(1)}, f32[2,64,1280]{2,1,0:T(8,128)}, u32[]{:S(2)}) copy-start(f32[2,64,1280]{2,1,0:T(8,128)} %slice.574) | copy-start | bytes 1966084
  51.5 16.8 %copy-start.2 = (f32[2,64,1280]{2,1,0:T(8,128)S(1)}, f32[2,64,1280]{2,1,0:T(8,128)}, u32[]{:S(2)}) copy-start(f32[2,64,1280]{2,1,0:T(8,128)} %copy-done.1) | copy-start | bytes 1966084
  51.5 104.7 %all-to-all-start = ((f32[32,4,1280]{2,1,0:T(4,128)}), f32[32,4,1280]{2,1,0:T(4,128)}, u32[]{:S(2)}, u32[]{:S(2)}) async-start(f32[32,4,1280]{2,1,0:T(4,128)} %broadcast_in_dim.26), calls=%async_computation | async-start | bytes 1310720 | tf_op jit(solution)/shard_map/all_to_all | solution.py:12
  82.3 4.4 %copy-start.15 = (f32[2,64,1280]{2,1,0:T(8,128)S(1)}, f32[2,64,1280]{2,1,0:T(8,128)}, u32[]{:S(2)}) copy-start(f32[2,64,1280]{2,1,0:T(8,128)} %slice.666) | copy-start | bytes 1966084
  82.3 4.4 %copy-start.16 = (f32[2,64,1280]{2,1,0:T(8,128)S(1)}, f32[2,64,1280]{2,1,0:T(8,128)}, u32[]{:S(2)}) copy-start(f32[2,64,1280]{2,1,0:T(8,128)} %slice.662) | copy-start | bytes 1966084
  97.3 1.3 copy-start.9
  97.3 1.5 copy-start.12
  102.2 1.1 copy-start.13
  104.8 10.9 %copy-start.7 = (f32[2,128,1280]{2,1,0:T(8,128)S(1)}, f32[2,128,1280]{2,1,0:T(8,128)}, u32[]{:S(2)}) copy-start(f32[2,128,1280]{2,1,0:T(8,128)} %add.450) | copy-start | bytes 3932164
  156.1 2.3 %copy-start.20 = (bf16[2,128,1280]{2,1,0:T(8,128)(2,1)S(1)}, bf16[2,128,1280]{2,1,0:T(8,128)(2,1)}, u32[]{:S(2)}) copy-start(bf16[2,128,1280]{2,1,0:T(8,128)(2,1)} %param.5) | copy-start | bytes 1966084
  156.2 2.2 %copy-start.5 = (f32[2,128,1280]{2,1,0:T(8,128)S(1)}, f32[2,128,1280]{2,1,0:T(8,128)}, u32[]{:S(2)}) copy-start(f32[2,128,1280]{2,1,0:T(8,128)} %copy-done.4) | copy-start | bytes 3932164
  156.2 2.2 %copy-start.6 = (f32[2,128,1280]{2,1,0:T(8,128)S(1)}, f32[2,128,1280]{2,1,0:T(8,128)}, u32[]{:S(2)}) copy-start(f32[2,128,1280]{2,1,0:T(8,128)} %pad.184) | copy-start | bytes 3932164
where the time goes:
time: 165 us; the launch traced here: 162 us
  local copies, waits for them, and re-layouts  83.6 us (51%)
  blocking collectives  33.7 us (20%)
  other arithmetic  30.2 us (18%)
  starting transfers between devices  13.5 us (8%)
    all_gather x3, blocking collectives, all_in_one(): both, at, found = (lax.all_gather(jnp.concatenate(lines), axis), 0, {})  33.7 us
    slice x44, local copies, waits for them, and re-layouts, body(): lax.associative_scan(join_pair, (keep, push), axis=1, reverse=True)  19.2 us
    rev x2, local copies, waits for them, and re-layouts, body(): lax.associative_scan(join_pair, (keep, push), axis=1, reverse=True)  17.4 us
    slice x44, local copies, waits for them, and re-layouts, body(): product, forward = lax.associative_scan(join_pair, (keep, push), axis=1)  17 us
    pad x24, local copies, waits for them, and re-layouts, body(): product, forward = lax.associative_scan(join_pair, (keep, push), axis=1)  14.8 us
    all_to_all x1, starting transfers between devices, from_everyone(): lax.all_to_all(jnp.broadcast_to(value[None], (peers, *value.shape)), axis...  13.5 us
    another operation x1, local copies, waits for them, and re-layouts  7.81 us
    add x13, other arithmetic, body(): product, forward = lax.associative_scan(join_pair, (keep, push), axis=1)  6.5 us
  transfers between devices with their start and end apart: 1, of which 0 were waited for; matrix products, arithmetic and copies ran while one was open for 34% of the time, Pallas kernels for 0%

commit v1 on v0

v1 whole, which is shorter than its diff:
```python
import jax
import jax.numpy as jnp
from jax import lax
from jax.experimental import pallas as pl
from jax.experimental.pallas import tpu as pltpu
from jax.sharding import Mesh
from jax.sharding import PartitionSpec as P

SPAN = ("span_0", "span_1", "span_2")
MESH = pl.DeviceIdType.MESH
TILE = 256
LANES = 128
DECAY, FORE, BACK = 0, 1, 2


def kernel(
    length, leak_hbm, signal_hbm, gate_hbm, out_ref,
    leak, signal, gate, keep_fore, keep_back, local, lower, upper, near, mid, far, enter,
    load_sem, gate_sem, send_x, recv_x, send_y, recv_y, send_z, recv_z,
):
    batch, steps, channels = leak.shape
    tiles, groups = channels // TILE, channels // LANES
    z, y, x = (lax.axis_index(name) for name in SPAN)
    axes = (("span_2", x, 2), ("span_1", y, 4), ("span_0", z, 4))

    def load(b, n, which):
        hbm, vmem = ((leak_hbm, leak), (signal_hbm, signal))[which]
        part = (b, slice(None), pl.ds(n * TILE, TILE))
        return pltpu.make_async_copy(hbm.at[part], vmem.at[part], load_sem.at[which, b, n])

    for b in range(batch):
        for n in range(tiles):
            load(b, n, 0).start()
            load(b, n, 1).start()
    gate_load = pltpu.make_async_copy(gate_hbm, gate, gate_sem)
    gate_load.start()

    barrier = pltpu.get_barrier_semaphore()
    for name, mine, size in axes:
        for d in range(1, size):
            pl.semaphore_signal(
                barrier, inc=1, device_id={name: lax.rem(mine + d, size)}, device_id_type=MESH
            )

    row = lax.broadcasted_iota(jnp.int32, (steps, 2 * steps), 0)
    column = lax.rem(lax.broadcasted_iota(jnp.int32, (steps, 2 * steps), 1), steps)
    lower[...] = jnp.where(column <= row, 1.0, 0.0).astype(jnp.bfloat16)
    upper[...] = jnp.where(column >= row, 1.0, 0.0).astype(jnp.bfloat16)

    scale = length ** (-0.5)
    for b in range(batch):
        for n in range(tiles):
            part = (b, slice(None), slice(n * TILE, (n + 1) * TILE))
            load(b, n, 0).wait()
            load(b, n, 1).wait()
            rate = leak[part]
            high = rate.astype(jnp.bfloat16)
            low = (rate - high.astype(jnp.float32)).astype(jnp.bfloat16)
            total = jnp.dot(
                lower[...], jnp.concatenate([high, low], 0), preferred_element_type=jnp.float32
            )
            upto = total * (1.0 / length)
            before = upto - rate * (1.0 / length)
            push = signal[part]
            push_wide = push.astype(jnp.float32)
            grown = (push_wide * (jnp.exp(upto) - 1.0)).astype(jnp.bfloat16)
            shrunk = (push_wide * (jnp.exp(-before) - 1.0)).astype(jnp.bfloat16)
            fore = jnp.dot(
                lower[...], jnp.concatenate([push, grown], 0), preferred_element_type=jnp.float32
            )
            back = jnp.dot(
                upper[...], jnp.concatenate([push, shrunk], 0), preferred_element_type=jnp.float32
            )
            down, up = jnp.exp(-upto), jnp.exp(before)
            fore, back = down * fore * scale, up * back * scale
            keep_fore[part] = down
            keep_back[part] = up
            local[part] = fore + back
            for h in range(TILE // LANES):
                at = b * groups + n * (TILE // LANES) + h
                lanes = slice(h * LANES, (h + 1) * LANES)
                near[x, DECAY, at : at + 1] = upto[steps - 1 :, lanes]
                near[x, FORE, at : at + 1] = fore[steps - 1 :, lanes]
                near[x, BACK, at : at + 1] = back[:1, lanes]

    pl.semaphore_wait(barrier, sum(size - 1 for _, _, size in axes))

    def pass_on(buffer, axis, d, q, slot, send, recv):
        name, mine, size = axis
        return pltpu.make_async_remote_copy(
            src_ref=buffer.at[mine, q],
            dst_ref=buffer.at[mine, q],
            send_sem=send.at[d - 1, slot],
            recv_sem=recv.at[mine, slot],
            device_id={name: lax.rem(mine + d, size)},
            device_id_type=MESH,
        )

    def arrived(buffer, axis, d, q, slot, send, recv):
        name, mine, size = axis
        source = lax.rem(mine + d, size)
        pltpu.make_async_remote_copy(
            src_ref=buffer.at[source, q],
            dst_ref=buffer.at[source, q],
            send_sem=send.at[d - 1, slot],
            recv_sem=recv.at[source, slot],
            device_id={name: source},
            device_id_type=MESH,
        ).wait_recv()

    order = (DECAY, FORE, BACK)
    sent_x = [pass_on(near, axes[0], 1, q, q, send_x, recv_x) for q in order]
    for copy in sent_x:
        copy.start()

    gate_load.wait()
    for b in range(batch):
        for n in range(tiles):
            part = (b, slice(None), slice(n * TILE, (n + 1) * TILE))
            g = gate[part].astype(jnp.float32)
            g = g / (1.0 + jnp.exp(-g))
            keep_fore[part] = keep_fore[part] * g
            keep_back[part] = keep_back[part] * g
            local[part] = local[part] * g

    sent_y, sent_z = [], []
    arrived(near, axes[0], 1, DECAY, DECAY, send_x, recv_x)
    decay = [near[s, DECAY] for s in range(2)]
    mid[y, DECAY] = decay[0] + decay[1]
    kept = [jnp.exp(-d) for d in decay]
    for q in order:
        if q == FORE:
            arrived(near, axes[0], 1, q, q, send_x, recv_x)
            earlier = near[0, FORE]
            mid[y, FORE] = earlier * kept[1] + near[1, FORE]
            carry_fore = jnp.where(x == 1, earlier, 0.0)
            reach_fore = jnp.where(x == 1, kept[0], 1.0)
        if q == BACK:
            arrived(near, axes[0], 1, q, q, send_x, recv_x)
            later = near[1, BACK]
            mid[y, BACK] = later * kept[0] + near[0, BACK]
            carry_back = jnp.where(x == 0, later, 0.0)
            reach_back = jnp.where(x == 0, kept[1], 1.0)
        for d in range(1, 4):
            copy = pass_on(mid, axes[1], d, q, q, send_y, recv_y)
            copy.start()
            sent_y.append(copy)

    for d in range(1, 4):
        arrived(mid, axes[1], d, DECAY, DECAY, send_y, recv_y)
    decay = [mid[s, DECAY] for s in range(4)]
    far[z, DECAY] = (decay[0] + decay[1]) + (decay[2] + decay[3])

    def onward(q, slot, wanted):
        for d in range(1, 4):
            target = lax.rem(z + d, 4)
            copy = pass_on(far, axes[2], d, q, slot, send_z, recv_z)
            if wanted is None:
                copy.start()
            else:
                pl.when(wanted(target))(copy.start)
            if slot == 0 or q == FORE:
                sent_z.append(copy)

    onward(DECAY, 0, None)
    kept = [jnp.exp(-d) for d in decay]
    for d in range(1, 4):
        arrived(mid, axes[1], d, FORE, FORE, send_y, recv_y)
    state, inside, reach = jnp.zeros_like(kept[0]), None, jnp.ones_like(kept[0])
    inside = state
    for s in range(4):
        inside = jnp.where(y == s, state, inside)
        reach = jnp.where(s < y, reach * kept[s], reach)
        state = state * kept[s] + mid[s, FORE]
    far[z, FORE] = state
    onward(FORE, 1, lambda target: target > z)
    carry_fore = carry_fore + reach_fore * inside
    reach_fore = reach_fore * reach
    for d in range(1, 4):
        arrived(mid, axes[1], d, BACK, BACK, send_y, recv_y)
    state, reach = jnp.zeros_like(kept[0]), jnp.ones_like(kept[0])
    inside = state
    for s in reversed(range(4)):
        inside = jnp.where(y == s, state, inside)
        reach = jnp.where(s > y, reach * kept[s], reach)
        state = state * kept[s] + mid[s, BACK]
    far[z, BACK] = state
    onward(BACK, 1, lambda target: target < z)
    carry_back = carry_back + reach_back * inside
    reach_back = reach_back * reach

    for d in range(1, 4):
        arrived(far, axes[2], d, DECAY, 0, send_z, recv_z)
    kept = [jnp.exp(-far[s, DECAY]) for s in range(4)]
    for d in range(1, 4):
        arrived(far, axes[2], d, FORE, 1, send_z, recv_z)
    state = jnp.zeros_like(kept[0])
    for s in range(4):
        state = jnp.where(s < z, state * kept[s] + far[s, FORE], state)
    enter[0] = carry_fore + reach_fore * state
    state = jnp.zeros_like(kept[0])
    for s in reversed(range(4)):
        state = jnp.where(s > z, state * kept[s] + far[s, BACK], state)
    enter[1] = (carry_back + reach_back * state) * jnp.exp(-near[x, DECAY])

    for b in range(batch):
        for n in range(groups):
            part = (b, slice(None), slice(n * LANES, (n + 1) * LANES))
            at = b * groups + n
            fore, back = enter[0, at : at + 1], enter[1, at : at + 1]
            gated = local[part] + (keep_fore[part] * fore + keep_back[part] * back)
            out_ref[part] = gated.astype(jnp.bfloat16)

    for copy in sent_x + sent_y + sent_z:
        copy.wait_send()


def solution(mesh):
    split = Mesh(
        mesh.devices.reshape(4, 4, 2, mesh.shape["cols"], mesh.shape["copy"]),
        ("span_0", "span_1", "span_2", "cols", "copy"),
    )

    def body(leak_rate, signal_in, gate_in):
        shape = leak_rate.shape
        batch, steps, channels = shape
        rows = batch * channels // LANES
        length = steps * lax.axis_size(SPAN)
        wide, narrow = pltpu.VMEM(shape, jnp.float32), pltpu.VMEM(shape, jnp.bfloat16)
        ends = pltpu.VMEM((4, 3, rows, LANES), jnp.float32)
        triangle = pltpu.VMEM((steps, 2 * steps), jnp.bfloat16)
        dma = pltpu.SemaphoreType.DMA
        return pl.pallas_call(
            lambda *refs: kernel(length, *refs),
            out_shape=jax.ShapeDtypeStruct(shape, jnp.bfloat16),
            in_specs=[pl.BlockSpec(memory_space=pl.ANY)] * 3,
            out_specs=pl.BlockSpec(memory_space=pltpu.VMEM),
            scratch_shapes=[
                wide, narrow, narrow, wide, wide, wide, triangle, triangle,
                pltpu.VMEM((2, 3, rows, LANES), jnp.float32), ends, ends,
                pltpu.VMEM((2, rows, LANES), jnp.float32),
                dma((2, batch, channels // TILE)), dma,
                dma((1, 3)), dma((2, 3)), dma((3, 3)), dma((4, 3)), dma((3, 2)), dma((4, 2)),
            ],
            compiler_params=pltpu.CompilerParams(collective_id=0, has_side_effects=True),
        )(leak_rate, signal_in, gate_in)

    placed = (P("copy", SPAN, "cols"),) * 3
    return jax.shard_map(
        body, mesh=split, in_specs=placed, out_specs=P("copy", SPAN, "cols"), check_vma=False
    )
```

time: 165 us -> 26.8 us (0.16); the launches traced: 162 us -> 26.7 us
  local copies, waits for them, and re-layouts: 83.6 us -> 1.97 us
  blocking collectives: 33.7 us -> 0 us
  other arithmetic: 30.2 us -> 0 us
  Pallas kernels: 0 us -> 24.7 us
  starting transfers between devices: 13.5 us -> 0 us
    slice x88 -> x0, local copies, waits for them, and re-layouts: 36.2 us -> none  [the longest x44 19.2 us: body(): lax.associative_scan(join_pair, (keep, push), axis=1, reverse=True)]
    all_gather x3 -> x0, blocking collectives: 33.7 us -> none  [all_in_one(): both, at, found = (lax.all_gather(jnp.concatenate(lines), axis), 0, {})]
    pallas_call x0 -> x1, Pallas kernels: none -> 24.7 us  [body(): pl.pallas_call(lambda *refs: kernel(length, *refs), out_shape=jax.ShapeDt...]
    pad x48 -> x0, local copies, waits for them, and re-layouts: 18.3 us -> none  [the longest x24 14.8 us: body(): product, forward = lax.associative_scan(join_pair, (keep, push), axis=1)]
    rev x2 -> x0, local copies, waits for them, and re-layouts: 17.4 us -> none  [body(): lax.associative_scan(join_pair, (keep, push), axis=1, reverse=True)]
    add x42 -> x0, other arithmetic: 16.4 us -> none  [the longest x13 6.5 us: body(): product, forward = lax.associative_scan(join_pair, (keep, push), axis=1)]
    all_to_all x1 -> x0, starting transfers between devices: 13.5 us -> none  [from_everyone(): lax.all_to_all(jnp.broadcast_to(value[None], (peers, *value.shape)), axis...]
    another operation x1 -> x0, local copies, waits for them, and re-layouts: 7.81 us -> none
  transfers between devices with their start and end apart: 1 -> 0, of which waited for: 0 -> 0; matrix products, arithmetic and copies ran while one was open for 34% -> 0% of each run, Pallas kernels for 0% -> 0%
where the time goes in v1:
time: 26.8 us; the launch traced here: 26.7 us
  Pallas kernels  24.7 us (92%)
  local copies, waits for them, and re-layouts  1.97 us (7%)
    pallas_call x1, Pallas kernels, body(): pl.pallas_call(lambda *refs: kernel(length, *refs), out_shape=jax.ShapeDt...  24.7 us
    unnamed x1, local copies, waits for them, and re-layouts  1.97 us

profile of v1, /device:TPU:2, one launch (start us, length us, event | category | flops | bytes accessed | tf_op | source)
XLA Modules:
  0.0 26.7 jit_solution(10266787038737688795)
XLA Ops:
  0.0 24.7 %shard_map.37 = bf16[2,128,1280]{2,1,0:T(8,128)(2,1)} custom-call(f32[2,128,1280]{2,1,0:T(8,128)} %refs_0_.1, bf16[2,128,1280]{2,1,0:T(8,128)(2,1)} %refs_1_.1, bf16[2,128,1280]{2,1,0:T(8,128)(2,1)} %refs_2_.1), custom_call_target="tpu_custom_call" | custom-call | tf_op jit(solution)/shard_map/pallas_call | solution.py:233
  24.7 2.0 %copy.5 = bf16[2,128,1280]{2,1,0:T(8,128)(2,1)} copy(bf16[2,128,1280]{2,1,0:T(8,128)(2,1)} %shard_map.37) | data formatting | bytes 1310720

commit v2 on v1

--- a/solution.py
+++ b/solution.py
@@ -232,7 +232,7 @@
         dma = pltpu.SemaphoreType.DMA
         return pl.pallas_call(
             lambda *refs: kernel(length, *refs),
-            out_shape=jax.ShapeDtypeStruct(shape, jnp.bfloat16),
+            out_shape=pltpu.VMEM(shape, jnp.bfloat16),
             in_specs=[pl.BlockSpec(memory_space=pl.ANY)] * 3,
             out_specs=pl.BlockSpec(memory_space=pltpu.VMEM),
             scratch_shapes=[

time: 26.8 us -> 24.8 us (0.925)
  local copies, waits for them, and re-layouts: 1.97 us -> 0.84 us
  Pallas kernels: 24.7 us -> 23.9 us
    unnamed x1, local copies, waits for them, and re-layouts: 1.97 us -> 0.84 us
    pallas_call x1, Pallas kernels: 24.7 us -> 23.9 us  [body(): pl.pallas_call(lambda *refs: kernel(length, *refs), out_shape=pltpu.VMEM(...]
where the time goes in v2:
time: 24.8 us; the launch traced here: 24.7 us
  Pallas kernels  23.9 us (96%)
  local copies, waits for them, and re-layouts  0.84 us (3%)
    pallas_call x1, Pallas kernels, body(): pl.pallas_call(lambda *refs: kernel(length, *refs), out_shape=pltpu.VMEM(...  23.9 us
    unnamed x1, local copies, waits for them, and re-layouts  0.84 us

profile of v2, /device:TPU:2, one launch (start us, length us, event | category | flops | bytes accessed | tf_op | source)
XLA Modules:
  0.0 24.7 jit_solution(4799428386987267734)
XLA Ops:
  0.0 23.9 %shard_map.37 = bf16[2,128,1280]{2,1,0:T(8,128)(2,1)S(1)} custom-call(f32[2,128,1280]{2,1,0:T(8,128)} %refs_0_.1, bf16[2,128,1280]{2,1,0:T(8,128)(2,1)} %refs_1_.1, bf16[2,128,1280]{2,1,0:T(8,128)(2,1)} %refs_2_.1), custom_call_target="tpu_custom_call" | custom-call | tf_op jit(solution)/shard_map/pallas_call | solution.py:233
  23.9 0.8 %copy.5 = bf16[2,128,1280]{2,1,0:T(8,128)(2,1)} copy(bf16[2,128,1280]{2,1,0:T(8,128)(2,1)S(1)} %shard_map.37) | data formatting | bytes 1310720

commit v3 on v2

v3 whole, which is shorter than its diff:
```python
import jax
import jax.numpy as jnp
from jax import lax
from jax.experimental import pallas as pl
from jax.experimental.pallas import tpu as pltpu
from jax.sharding import Mesh
from jax.sharding import PartitionSpec as P

SPAN = ("span_0", "span_1", "span_2")
MESH = pl.DeviceIdType.MESH
TILE, LANES, GROUP = 256, 128, 640
FORE, DECAY, BACK = 0, 1, 2
AROUND = ((2, 1), (1, 1), (3, 1), (2, 0), (0, 1), (1, 0), (3, 0))


def kernel(
    length, leak_hbm, signal_hbm, gate_hbm, out_ref,
    leak, signal, gate, upto_ref, keep_fore, keep_back, local, lower, upper, near, far, enter,
    load_sem, gate_sem, send_near, recv_near, send_far, recv_far,
):
    batch, steps, channels = leak.shape
    groups = channels // LANES
    z, y, x = (lax.axis_index(name) for name in SPAN)
    me = y * 2 + x
    parts = [
        (b, slice(None), slice(c, c + GROUP)) for b in range(batch) for c in range(0, channels, GROUP)
    ]

    def loads(k):
        return [
            pltpu.make_async_copy(hbm.at[parts[k]], vmem.at[parts[k]], load_sem.at[which, k])
            for which, (hbm, vmem) in enumerate(((leak_hbm, leak), (signal_hbm, signal)))
        ]

    for k in range(len(parts)):
        for copy in loads(k):
            copy.start()
    gate_load = pltpu.make_async_copy(gate_hbm, gate, gate_sem)
    gate_load.start()

    def beside(dy, dx):
        return lax.rem(y + dy, 4), lax.rem(x + dx, 2)

    barrier = pltpu.get_barrier_semaphore()
    for dy, dx in AROUND:
        there = beside(dy, dx)
        pl.semaphore_signal(
            barrier, inc=1, device_id={"span_1": there[0], "span_2": there[1]}, device_id_type=MESH
        )
    for d in range(1, 4):
        pl.semaphore_signal(
            barrier, inc=1, device_id={"span_0": lax.rem(z + d, 4)}, device_id_type=MESH
        )

    row = lax.broadcasted_iota(jnp.int32, (steps, 2 * steps), 0)
    column = lax.rem(lax.broadcasted_iota(jnp.int32, (steps, 2 * steps), 1), steps)
    lower[...] = jnp.where(column <= row, 1.0, 0.0).astype(jnp.bfloat16)
    upper[...] = jnp.where(column >= row, 1.0, 0.0).astype(jnp.bfloat16)

    scale = length ** (-0.5)

    def add_up(k):
        rate = leak[parts[k]]
        high = rate.astype(jnp.bfloat16)
        low = (rate - high.astype(jnp.float32)).astype(jnp.bfloat16)
        total = jnp.dot(
            lower[...], jnp.concatenate([high, low], 0), preferred_element_type=jnp.float32
        )
        upto_ref[parts[k]] = total * (1.0 / length)

    def summarize(k):
        upto = upto_ref[parts[k]]
        before = upto - leak[parts[k]] * (1.0 / length)
        push = signal[parts[k]].astype(jnp.float32)
        last = upto[steps - 1 :]
        fore = jnp.sum(jnp.exp(upto) * push, 0, keepdims=True) * (jnp.exp(-last) * scale)
        back = jnp.sum(jnp.exp(-before) * push, 0, keepdims=True) * scale
        for h in range(GROUP // LANES):
            at = k * (GROUP // LANES) + h
            lanes = slice(h * LANES, (h + 1) * LANES)
            near[me, DECAY, at : at + 1] = last[:, lanes]
            near[me, FORE, at : at + 1] = fore[:, lanes]
            near[me, BACK, at : at + 1] = back[:, lanes]

    for k in range(len(parts)):
        for copy in loads(k):
            copy.wait()
        add_up(k)
        if k:
            summarize(k - 1)
    summarize(len(parts) - 1)

    pl.semaphore_wait(barrier, len(AROUND) + 3)

    def to_slab(i, planes, kind):
        there = beside(*AROUND[i])
        return pltpu.make_async_remote_copy(
            src_ref=near.at[me, planes],
            dst_ref=near.at[me, planes],
            send_sem=send_near.at[i, kind],
            recv_sem=recv_near.at[me, kind],
            device_id={"span_1": there[0], "span_2": there[1]},
            device_id_type=MESH,
        )

    def from_slab(i, planes, kind):
        there = beside(*AROUND[i])
        at = there[0] * 2 + there[1]
        pltpu.make_async_remote_copy(
            src_ref=near.at[at, planes],
            dst_ref=near.at[at, planes],
            send_sem=send_near.at[i, kind],
            recv_sem=recv_near.at[at, kind],
            device_id={"span_1": there[0], "span_2": there[1]},
            device_id_type=MESH,
        ).wait_recv()

    first, second = pl.ds(DECAY, 2), pl.ds(FORE, 1)
    sent = [to_slab(i, first, 0) for i in range(len(AROUND))]
    sent += [to_slab(i, second, 1) for i in range(len(AROUND))]
    for copy in sent:
        copy.start()

    gate_load.wait()
    for b in range(batch):
        for c in range(0, channels, TILE):
            part = (b, slice(None), slice(c, c + TILE))
            upto = upto_ref[part]
            before = upto - leak[part] * (1.0 / length)
            push = signal[part]
            push_wide = push.astype(jnp.float32)
            grown = (push_wide * (jnp.exp(upto) - 1.0)).astype(jnp.bfloat16)
            shrunk = (push_wide * (jnp.exp(-before) - 1.0)).astype(jnp.bfloat16)
            fore = jnp.dot(
                lower[...], jnp.concatenate([push, grown], 0), preferred_element_type=jnp.float32
            )
            back = jnp.dot(
                upper[...], jnp.concatenate([push, shrunk], 0), preferred_element_type=jnp.float32
            )
            g = gate[part].astype(jnp.float32)
            g = g / (1.0 + jnp.exp(-g))
            down, up = jnp.exp(-upto) * g, jnp.exp(before) * g
            keep_fore[part] = down
            keep_back[part] = up
            local[part] = (down * fore + up * back) * scale

    def to_slabs(d, planes):
        return pltpu.make_async_remote_copy(
            src_ref=far.at[z, planes],
            dst_ref=far.at[z, planes],
            send_sem=send_far.at[d - 1],
            recv_sem=recv_far.at[z],
            device_id={"span_0": lax.rem(z + d, 4)},
            device_id_type=MESH,
        )

    for i in range(len(AROUND)):
        from_slab(i, first, 0)
    decay = [near[s, DECAY] for s in range(8)]
    kept = [jnp.exp(-d) for d in decay]
    zero = jnp.zeros_like(kept[0])
    state = inside_back = zero
    for s in reversed(range(8)):
        inside_back = jnp.where(me == s, state, inside_back)
        state = state * kept[s] + near[s, BACK]
    far[z, BACK] = state
    far[z, DECAY] = sum(decay[1:], decay[0])
    for d in range(1, 4):
        pl.when(lax.rem(z + d, 4) < z)(to_slabs(d, pl.ds(DECAY, 2)).start)

    for i in range(len(AROUND)):
        from_slab(i, second, 1)
    state = inside_fore = zero
    for s in range(8):
        inside_fore = jnp.where(me == s, state, inside_fore)
        state = state * kept[s] + near[s, FORE]
    far[z, FORE] = state
    for d in range(1, 4):
        pl.when(lax.rem(z + d, 4) > z)(to_slabs(d, pl.ds(FORE, 2)).start)

    ahead = behind = zero
    for s in range(8):
        ahead = jnp.where(me > s, ahead + decay[s], ahead)
        behind = jnp.where(me < s, behind + decay[s], behind)
    own = jnp.exp(-near[me, DECAY])
    reach_fore, reach_back = jnp.exp(-ahead), jnp.exp(-behind) * own
    inside_back = inside_back * own

    for d in range(1, 4):
        source = lax.rem(z + d, 4)
        pltpu.make_async_remote_copy(
            src_ref=far.at[source, pl.ds(DECAY, 2)],
            dst_ref=far.at[source, pl.ds(DECAY, 2)],
            send_sem=send_far.at[d - 1],
            recv_sem=recv_far.at[source],
            device_id={"span_0": source},
            device_id_type=MESH,
        ).wait_recv()
    kept = [jnp.exp(-far[s, DECAY]) for s in range(4)]
    state = zero
    for s in range(4):
        state = jnp.where(s < z, state * kept[s] + far[s, FORE], state)
    enter[0] = inside_fore + reach_fore * state
    state = zero
    for s in reversed(range(4)):
        state = jnp.where(s > z, state * kept[s] + far[s, BACK], state)
    enter[1] = inside_back + reach_back * state

    for b in range(batch):
        for n in range(groups):
            part = (b, slice(None), slice(n * LANES, (n + 1) * LANES))
            at = b * groups + n
            fore, back = enter[0, at : at + 1], enter[1, at : at + 1]
            gated = local[part] + (keep_fore[part] * fore + keep_back[part] * back)
            out_ref[part] = gated.astype(jnp.bfloat16)

    for copy in sent:
        copy.wait_send()
    for d in range(1, 4):
        to_slabs(d, pl.ds(DECAY, 2)).wait_send()


def solution(mesh):
    split = Mesh(
        mesh.devices.reshape(4, 4, 2, mesh.shape["cols"], mesh.shape["copy"]),
        ("span_0", "span_1", "span_2", "cols", "copy"),
    )

    def body(leak_rate, signal_in, gate_in):
        shape = leak_rate.shape
        batch, steps, channels = shape
        rows = batch * channels // LANES
        length = steps * lax.axis_size(SPAN)
        wide, narrow = pltpu.VMEM(shape, jnp.float32), pltpu.VMEM(shape, jnp.bfloat16)
        triangle = pltpu.VMEM((steps, 2 * steps), jnp.bfloat16)
        dma = pltpu.SemaphoreType.DMA
        return pl.pallas_call(
            lambda *refs: kernel(length, *refs),
            out_shape=pltpu.VMEM(shape, jnp.bfloat16),
            in_specs=[pl.BlockSpec(memory_space=pl.ANY)] * 3,
            out_specs=pl.BlockSpec(memory_space=pltpu.VMEM),
            scratch_shapes=[
                wide, narrow, narrow, wide, wide, wide, wide, triangle, triangle,
                pltpu.VMEM((8, 3, rows, LANES), jnp.float32),
                pltpu.VMEM((4, 3, rows, LANES), jnp.float32),
                pltpu.VMEM((2, rows, LANES), jnp.float32),
                dma((2, batch * channels // GROUP)), dma,
                dma((len(AROUND), 2)), dma((8, 2)), dma((3,)), dma((4,)),
            ],
            compiler_params=pltpu.CompilerParams(collective_id=0, has_side_effects=True),
        )(leak_rate, signal_in, gate_in)

    placed = (P("copy", SPAN, "cols"),) * 3
    return jax.shard_map(
        body, mesh=split, in_specs=placed, out_specs=P("copy", SPAN, "cols"), check_vma=False
    )
```

time: 24.8 us -> 20.3 us (0.82)
  Pallas kernels: 23.9 us -> 19.3 us
    pallas_call x1, Pallas kernels: 23.9 us -> 19.3 us  [body(): pl.pallas_call(lambda *refs: kernel(length, *refs), out_shape=pltpu.VMEM(...]
where the time goes in v3:
time: 20.3 us; the launch traced here: 20.2 us
  Pallas kernels  19.3 us (95%)
  local copies, waits for them, and re-layouts  0.84 us (4%)
    pallas_call x1, Pallas kernels, body(): pl.pallas_call(lambda *refs: kernel(length, *refs), out_shape=pltpu.VMEM(...  19.3 us
    unnamed x1, local copies, waits for them, and re-layouts  0.84 us

profile of v3, /device:TPU:2, one launch (start us, length us, event | category | flops | bytes accessed | tf_op | source)
XLA Modules:
  0.0 20.2 jit_solution(4519042843305466935)
XLA Ops:
  0.0 19.3 %shard_map.37 = bf16[2,128,1280]{2,1,0:T(8,128)(2,1)S(1)} custom-call(f32[2,128,1280]{2,1,0:T(8,128)} %refs_0_.1, bf16[2,128,1280]{2,1,0:T(8,128)(2,1)} %refs_1_.1, bf16[2,128,1280]{2,1,0:T(8,128)(2,1)} %refs_2_.1), custom_call_target="tpu_custom_call" | custom-call | tf_op jit(solution)/shard_map/pallas_call | solution.py:237
  19.3 0.8 %copy.5 = bf16[2,128,1280]{2,1,0:T(8,128)(2,1)} copy(bf16[2,128,1280]{2,1,0:T(8,128)(2,1)S(1)} %shard_map.37) | data formatting | bytes 1310720

commit v4 on v3

v4 whole, which is shorter than its diff:
```python
import math

import jax
import jax.numpy as jnp
from jax import lax
from jax.experimental import pallas as pl
from jax.experimental.pallas import tpu as pltpu
from jax.sharding import Mesh
from jax.sharding import PartitionSpec as P

SPAN = ("slab", "place")
MESH = pl.DeviceIdType.MESH
TILE, LANES, GROUP = 256, 128, 640
FORE, DECAY, BACK = 0, 1, 2


def kernel(
    length, leak_hbm, signal_hbm, gate_hbm, out_ref,
    leak, signal, gate, since_ref, keep_fore, keep_back, local, ahead_of, lower, upper, near, far, enter,
    load_sem, near_sem, far_sem,
):
    batch, steps, channels = leak.shape
    groups = channels // LANES
    z, me = lax.axis_index("slab"), lax.axis_index("place")
    parts = [
        (b, slice(None), slice(c, c + GROUP)) for b in range(batch) for c in range(0, channels, GROUP)
    ]

    def load(which, k):
        hbm, vmem = ((leak_hbm, leak), (signal_hbm, signal))[which]
        return pltpu.make_async_copy(hbm.at[parts[k]], vmem.at[parts[k]], load_sem.at[which, k])

    for k in range(len(parts)):
        for which in range(2):
            load(which, k).start()
    gate_load = pltpu.make_async_copy(gate_hbm, gate, load_sem.at[0, 0])
    barrier = pltpu.get_barrier_semaphore()
    for d in range(1, 8):
        pl.semaphore_signal(
            barrier, inc=1, device_id={"place": lax.rem(me + d, 8)}, device_id_type=MESH
        )
    for d in range(1, 4):
        pl.semaphore_signal(
            barrier, inc=1, device_id={"slab": lax.rem(z + d, 4)}, device_id_type=MESH
        )

    row = lax.broadcasted_iota(jnp.int32, (steps, 2 * steps), 0)
    column = lax.rem(lax.broadcasted_iota(jnp.int32, (steps, 2 * steps), 1), steps)
    ahead_of[...] = jnp.where(column < row, -1.0, 0.0).astype(jnp.bfloat16)
    lower[...] = jnp.where(column <= row, 1.0, 0.0).astype(jnp.bfloat16)
    upper[...] = jnp.where(column >= row, 1.0, 0.0).astype(jnp.bfloat16)

    scale = length ** (-0.5)
    rate_scale = math.log2(math.e) / length

    def add_up(k):
        rate = leak[parts[k]]
        high = rate.astype(jnp.bfloat16)
        low = (rate - high.astype(jnp.float32)).astype(jnp.bfloat16)
        total = jnp.dot(
            ahead_of[...], jnp.concatenate([high, low], 0), preferred_element_type=jnp.float32
        )
        since_ref[parts[k]] = total * rate_scale

    def summarize(k):
        b, _, columns = parts[k]
        for h in range(GROUP // LANES):
            at = k * (GROUP // LANES) + h
            start = columns.start + h * LANES
            lanes = slice(start, start + LANES)
            back = jnp.zeros((8, LANES), jnp.float32)
            for r in range(0, steps, 16):
                piece = (b, slice(r, r + 16), lanes)
                reached = jnp.exp2(since_ref[piece]) * signal[piece].astype(jnp.float32)
                back = back + (reached[:8] + reached[8:])
            end = (b, slice(steps - 1, steps), lanes)
            near[me, DECAY, at : at + 1] = leak[end] * rate_scale - since_ref[end]
            near[me, BACK, at : at + 1] = jnp.sum(back, 0, keepdims=True) * scale

    for k in range(len(parts)):
        load(0, k).wait()
        load(1, k).wait()
        add_up(k)
        if k:
            summarize(k - 1)
    summarize(len(parts) - 1)
    gate_load.start()

    pl.semaphore_wait(barrier, 10)

    def within(i, planes, kind):
        return pltpu.make_async_remote_copy(
            src_ref=near.at[me, planes],
            dst_ref=near.at[me, planes],
            send_sem=near_sem.at[2],
            recv_sem=near_sem.at[kind],
            device_id={"place": i},
            device_id_type=MESH,
        )

    def all_within(planes, kind):
        part = near.at[pl.ds(0, 7), planes]
        return pltpu.make_async_remote_copy(
            src_ref=part,
            dst_ref=part,
            send_sem=near_sem.at[2],
            recv_sem=near_sem.at[kind],
            device_id={"place": me},
            device_id_type=MESH,
        )

    first, second = pl.ds(DECAY, 2), pl.ds(FORE, 1)
    for k in range(7):
        within(k + lax.div(k - me + 8, 8), first, 0).start()

    gate_load.wait()
    for b in range(batch):
        for c in range(0, channels, TILE):
            part = (b, slice(None), slice(c, c + TILE))
            since = since_ref[part]
            upto = leak[part] * rate_scale - since
            push = signal[part]
            push_wide = push.astype(jnp.float32)
            growth = jnp.exp2(upto)
            reached = jnp.sum(growth * push_wide, 0, keepdims=True)
            for h in range(TILE // LANES):
                at = b * groups + c // LANES + h
                near[me, FORE, at : at + 1] = reached[:, h * LANES : (h + 1) * LANES]
            grown = (push_wide * (growth - 1.0)).astype(jnp.bfloat16)
            shrunk = (push_wide * (jnp.exp2(since) - 1.0)).astype(jnp.bfloat16)
            fore = jnp.dot(
                lower[...], jnp.concatenate([push, grown], 0), preferred_element_type=jnp.float32
            )
            back = jnp.dot(
                upper[...], jnp.concatenate([push, shrunk], 0), preferred_element_type=jnp.float32
            )
            g = gate[part].astype(jnp.float32)
            g = g / (1.0 + jnp.exp(-g))
            down, up = jnp.exp2(-upto) * g, jnp.exp2(-since) * g
            keep_fore[part] = down
            keep_back[part] = up
            local[part] = (down * fore + up * back) * scale

    own = jnp.exp2(-near[me, DECAY])
    near[me, FORE] = near[me, FORE] * (own * scale)
    for k in range(7):
        within(k + lax.div(k - me + 8, 8), second, 1).start()

    def across(i, planes):
        return pltpu.make_async_remote_copy(
            src_ref=far.at[z, planes],
            dst_ref=far.at[z, planes],
            send_sem=far_sem.at[0],
            recv_sem=far_sem.at[1],
            device_id={"slab": i},
            device_id_type=MESH,
        )

    all_within(first, 0).wait_recv()
    decay = [near[s, DECAY] for s in range(8)]
    kept = [jnp.exp2(-d) for d in decay]
    zero = jnp.zeros_like(kept[0])
    state = inside_back = zero
    for s in reversed(range(8)):
        inside_back = jnp.where(me == s, state, inside_back)
        state = state * kept[s] + near[s, BACK]
    far[z, BACK] = state
    far[z, DECAY] = sum(decay[1:], decay[0])
    for i in range(3):
        pl.when(i < z)(across(i, pl.ds(DECAY, 2)).start)

    all_within(second, 1).wait_recv()
    state = inside_fore = zero
    for s in range(8):
        inside_fore = jnp.where(me == s, state, inside_fore)
        state = state * kept[s] + near[s, FORE]
    far[z, FORE] = state
    for i in range(1, 4):
        pl.when(i > z)(across(i, pl.ds(FORE, 2)).start)

    ahead = behind = zero
    for s in range(8):
        ahead = jnp.where(me > s, ahead + decay[s], ahead)
        behind = jnp.where(me < s, behind + decay[s], behind)
    reach_fore, reach_back = jnp.exp2(-ahead), jnp.exp2(-behind) * own
    inside_back = inside_back * own
    all_within(slice(None), 0).wait_send()

    three = far.at[pl.ds(0, 2)]
    all_across = pltpu.make_async_remote_copy(
        src_ref=three,
        dst_ref=three,
        send_sem=far_sem.at[0],
        recv_sem=far_sem.at[1],
        device_id={"slab": z},
        device_id_type=MESH,
    )
    all_across.wait_recv()
    kept = [jnp.exp2(-far[s, DECAY]) for s in range(4)]
    state = zero
    for s in range(4):
        state = jnp.where(s < z, state * kept[s] + far[s, FORE], state)
    enter[0] = inside_fore + reach_fore * state
    state = zero
    for s in reversed(range(4)):
        state = jnp.where(s > z, state * kept[s] + far[s, BACK], state)
    enter[1] = inside_back + reach_back * state

    for b in range(batch):
        for n in range(groups):
            part = (b, slice(None), slice(n * LANES, (n + 1) * LANES))
            at = b * groups + n
            fore, back = enter[0, at : at + 1], enter[1, at : at + 1]
            gated = local[part] + (keep_fore[part] * fore + keep_back[part] * back)
            out_ref[part] = gated.astype(jnp.bfloat16)

    all_across.wait_send()


def solution(mesh):
    split = Mesh(
        mesh.devices.reshape(4, 8, mesh.shape["cols"], mesh.shape["copy"]),
        ("slab", "place", "cols", "copy"),
    )

    def body(leak_rate, signal_in, gate_in):
        shape = leak_rate.shape
        batch, steps, channels = shape
        rows = batch * channels // LANES
        length = steps * lax.axis_size(SPAN)
        wide, narrow = pltpu.VMEM(shape, jnp.float32), pltpu.VMEM(shape, jnp.bfloat16)
        triangle = pltpu.VMEM((steps, 2 * steps), jnp.bfloat16)
        dma = pltpu.SemaphoreType.DMA
        return pl.pallas_call(
            lambda *refs: kernel(length, *refs),
            out_shape=pltpu.VMEM(shape, jnp.bfloat16),
            in_specs=[pl.BlockSpec(memory_space=pl.ANY)] * 3,
            out_specs=pl.BlockSpec(memory_space=pltpu.VMEM),
            scratch_shapes=[
                wide, narrow, narrow, wide, wide, wide, wide, triangle, triangle, triangle,
                pltpu.VMEM((8, 3, rows, LANES), jnp.float32),
                pltpu.VMEM((4, 3, rows, LANES), jnp.float32),
                pltpu.VMEM((2, rows, LANES), jnp.float32),
                dma((2, batch * channels // GROUP)), dma((3,)), dma((2,)),
            ],
            compiler_params=pltpu.CompilerParams(collective_id=0, has_side_effects=True),
        )(leak_rate, signal_in, gate_in)

    placed = (P("copy", SPAN, "cols"),) * 3
    return jax.shard_map(
        body, mesh=split, in_specs=placed, out_specs=P("copy", SPAN, "cols"), check_vma=False
    )
```

time: 20.3 us -> 19.6 us (0.966)
  the two profiles are of different devices: /device:TPU:2 before, /device:TPU:26 now
where the time goes in v4:
time: 19.6 us; the launch traced here: 19.5 us
  Pallas kernels  18.6 us (95%)
  local copies, waits for them, and re-layouts  0.84 us (4%)
    pallas_call x1, Pallas kernels, body(): pl.pallas_call(lambda *refs: kernel(length, *refs), out_shape=pltpu.VMEM(...  18.6 us
    unnamed x1, local copies, waits for them, and re-layouts  0.84 us

profile of v4, /device:TPU:26, one launch (start us, length us, event | category | flops | bytes accessed | tf_op | source)
XLA Modules:
  0.0 19.5 jit_solution(14714465527218825763)
XLA Ops:
  0.0 18.6 %shard_map.37 = bf16[2,128,1280]{2,1,0:T(8,128)(2,1)S(1)} custom-call(f32[2,128,1280]{2,1,0:T(8,128)} %refs_0_.1, bf16[2,128,1280]{2,1,0:T(8,128)(2,1)} %refs_1_.1, bf16[2,128,1280]{2,1,0:T(8,128)(2,1)} %refs_2_.1), custom_call_target="tpu_custom_call" | custom-call | tf_op jit(solution)/shard_map/pallas_call | solution.py:234
  18.6 0.8 %copy.5 = bf16[2,128,1280]{2,1,0:T(8,128)(2,1)} copy(bf16[2,128,1280]{2,1,0:T(8,128)(2,1)S(1)} %shard_map.37) | data formatting | bytes 1310720

commit v5 on v4

--- a/solution.py
+++ b/solution.py
@@ -10,14 +10,16 @@
 
 SPAN = ("slab", "place")
 MESH = pl.DeviceIdType.MESH
-TILE, LANES, GROUP = 256, 128, 640
+TILE, LANES, GROUP, CHUNK = 256, 128, 640, 2
 FORE, DECAY, BACK = 0, 1, 2
 
+AROUND = ((2, 1), (1, 1), (3, 1), (2, 0), (0, 1), (1, 0), (3, 0))
+
 
 def kernel(
-    length, leak_hbm, signal_hbm, gate_hbm, out_ref,
-    leak, signal, gate, since_ref, keep_fore, keep_back, local, ahead_of, lower, upper, near, far, enter,
-    load_sem, near_sem, far_sem,
+    length, leak_hbm, signal_hbm, gate_hbm, enter, keep_fore, keep_back, local,
+    leak, signal, gate, since_ref, ahead_of, lower, upper, near, far,
+    load_sem, near_sem, far_sem, later_sem,
 ):
     batch, steps, channels = leak.shape
     groups = channels // LANES
@@ -39,10 +41,12 @@
         pl.semaphore_signal(
             barrier, inc=1, device_id={"place": lax.rem(me + d, 8)}, device_id_type=MESH
         )
-    for d in range(1, 4):
-        pl.semaphore_signal(
-            barrier, inc=1, device_id={"slab": lax.rem(z + d, 4)}, device_id_type=MESH
-        )
+    for i in range(1, 4):
+
+        @pl.when(i > z)
+        def _():
+            pl.semaphore_signal(barrier, inc=1, device_id={"slab": i}, device_id_type=MESH)
+
 
     row = lax.broadcasted_iota(jnp.int32, (steps, 2 * steps), 0)
     column = lax.rem(lax.broadcasted_iota(jnp.int32, (steps, 2 * steps), 1), steps)
@@ -86,7 +90,7 @@
     summarize(len(parts) - 1)
     gate_load.start()
 
-    pl.semaphore_wait(barrier, 10)
+    pl.semaphore_wait(barrier, 7 + z)
 
     def within(i, planes, kind):
         return pltpu.make_async_remote_copy(
@@ -110,8 +114,16 @@
         )
 
     first, second = pl.ds(DECAY, 2), pl.ds(FORE, 1)
-    for k in range(7):
-        within(k + lax.div(k - me + 8, 8), first, 0).start()
+    y, x = lax.div(me, 2), lax.rem(me, 2)
+    others = [lax.rem(y + dy, 4) * 2 + lax.rem(x + dx, 2) for dy, dx in AROUND]
+
+    def to_slab(planes, kind):
+        for i in range(2):
+            pl.when(i != me)(within(i, planes, kind).start)
+        for i in others:
+            pl.when(i > 1)(within(i, planes, kind).start)
+
+    to_slab(first, 0)
 
     gate_load.wait()
     for b in range(batch):
@@ -143,8 +155,7 @@
 
     own = jnp.exp2(-near[me, DECAY])
     near[me, FORE] = near[me, FORE] * (own * scale)
-    for k in range(7):
-        within(k + lax.div(k - me + 8, 8), second, 1).start()
+    to_slab(second, 1)
 
     def across(i, planes):
         return pltpu.make_async_remote_copy(
@@ -168,6 +179,14 @@
     far[z, DECAY] = sum(decay[1:], decay[0])
     for i in range(3):
         pl.when(i < z)(across(i, pl.ds(DECAY, 2)).start)
+    for i in range(3):
+
+        @pl.when(i < z)
+        def _():
+            pl.semaphore_signal(
+                later_sem.at[jnp.where(i == z - 1, 0, 1)],
+                inc=1, device_id={"slab": i}, device_id_type=MESH,
+            )
 
     all_within(second, 1).wait_recv()
     state = inside_fore = zero
@@ -175,8 +194,18 @@
         inside_fore = jnp.where(me == s, state, inside_fore)
         state = state * kept[s] + near[s, FORE]
     far[z, FORE] = state
-    for i in range(1, 4):
-        pl.when(i > z)(across(i, pl.ds(FORE, 2)).start)
+
+    @pl.when(z < 3)
+    def _():
+        pl.semaphore_wait(later_sem.at[0], 1)
+        across(lax.rem(z + 1, 4), pl.ds(FORE, 2)).start()
+
+    @pl.when(z < 2)
+    def _():
+        pl.semaphore_wait(later_sem.at[1], 2 - z)
+
+    for i in range(2, 4):
+        pl.when(i > z + 1)(across(i, pl.ds(FORE, 2)).start)
 
     ahead = behind = zero
     for s in range(8):
@@ -206,15 +235,26 @@
         state = jnp.where(s > z, state * kept[s] + far[s, BACK], state)
     enter[1] = inside_back + reach_back * state
 
-    for b in range(batch):
-        for n in range(groups):
-            part = (b, slice(None), slice(n * LANES, (n + 1) * LANES))
-            at = b * groups + n
-            fore, back = enter[0, at : at + 1], enter[1, at : at + 1]
-            gated = local[part] + (keep_fore[part] * fore + keep_back[part] * back)
-            out_ref[part] = gated.astype(jnp.bfloat16)
-
     all_across.wait_send()
+
+
+def finish(enter, keep_fore, keep_back, local, out_hbm, out, sem):
+    batch, _, channels = out.shape
+    groups = channels // LANES
+
+    def store(b, first, last):
+        part = (b, slice(None), slice(first * LANES, last * LANES))
+        return pltpu.make_async_copy(out.at[part], out_hbm.at[part], sem)
+
+    for at in range(batch * groups):
+        b, n = divmod(at, groups)
+        part = (b, slice(None), slice(n * LANES, (n + 1) * LANES))
+        fore, back = enter[0, at : at + 1], enter[1, at : at + 1]
+        gated = local[part] + (keep_fore[part] * fore + keep_back[part] * back)
+        out[part] = gated.astype(jnp.bfloat16)
+        if n % CHUNK == CHUNK - 1:
+            store(b, n + 1 - CHUNK, n + 1).start()
+    pltpu.make_async_copy(out, out_hbm, sem).wait()
 
 
 def solution(mesh):
@@ -231,20 +271,33 @@
         wide, narrow = pltpu.VMEM(shape, jnp.float32), pltpu.VMEM(shape, jnp.bfloat16)
         triangle = pltpu.VMEM((steps, 2 * steps), jnp.bfloat16)
         dma = pltpu.SemaphoreType.DMA
-        return pl.pallas_call(
+        wide_out = pltpu.VMEM(shape, jnp.float32)
+        entering = pltpu.VMEM((2, rows, LANES), jnp.float32)
+        vmem = pl.BlockSpec(memory_space=pltpu.VMEM)
+        states = pl.pallas_call(
             lambda *refs: kernel(length, *refs),
-            out_shape=pltpu.VMEM(shape, jnp.bfloat16),
+            out_shape=[entering, wide_out, wide_out, wide_out],
             in_specs=[pl.BlockSpec(memory_space=pl.ANY)] * 3,
-            out_specs=pl.BlockSpec(memory_space=pltpu.VMEM),
+            out_specs=[vmem] * 4,
             scratch_shapes=[
-                wide, narrow, narrow, wide, wide, wide, wide, triangle, triangle, triangle,
+                wide, narrow, narrow, wide, triangle, triangle, triangle,
                 pltpu.VMEM((8, 3, rows, LANES), jnp.float32),
                 pltpu.VMEM((4, 3, rows, LANES), jnp.float32),
-                pltpu.VMEM((2, rows, LANES), jnp.float32),
                 dma((2, batch * channels // GROUP)), dma((3,)), dma((2,)),
+                pltpu.SemaphoreType.REGULAR((2,)),
             ],
-            compiler_params=pltpu.CompilerParams(collective_id=0, has_side_effects=True),
+            compiler_params=pltpu.CompilerParams(
+                collective_id=0, has_side_effects=True, vmem_limit_bytes=62_600_000
+            ),
         )(leak_rate, signal_in, gate_in)
+        return pl.pallas_call(
+            finish,
+            out_shape=jax.ShapeDtypeStruct(shape, jnp.bfloat16),
+            in_specs=[vmem] * 4,
+            out_specs=pl.BlockSpec(memory_space=pl.ANY),
+            scratch_shapes=[narrow, dma],
+            compiler_params=pltpu.CompilerParams(vmem_limit_bytes=32 << 20),
+        )(*states)
 
     placed = (P("copy", SPAN, "cols"),) * 3
     return jax.shard_map(

time: 19.6 us -> 19.1 us (0.974)
  the two profiles are of different devices: /device:TPU:26 before, /device:TPU:2 now
where the time goes in v5:
time: 19.1 us; the launch traced here: 18.9 us
  Pallas kernels  18.9 us (99%)
    pallas_call x1, Pallas kernels, body(): pl.pallas_call(lambda *refs: kernel(length, *refs), out_shape=[entering,...  18 us
    pallas_call x1, Pallas kernels, body(): pl.pallas_call(finish, out_shape=jax.ShapeDtypeStruct(shape, jnp.bfloat16...  0.86 us

profile of v5, /device:TPU:2, one launch (start us, length us, event | category | flops | bytes accessed | tf_op | source)
XLA Modules:
  0.0 18.9 jit_solution(5075634431826136923)
XLA Ops:
  0.0 18.0 %shard_map.37 = (f32[2,20,128]{2,1,0:T(8,128)S(1)}, f32[2,128,1280]{2,1,0:T(8,128)S(1)}, f32[2,128,1280]{2,1,0:T(8,128)S(1)}, f32[2,128,1280]{2,1,0:T(8,128)S(1)}) custom-call(f32[2,128,1280]{2,1,0:T(8,128)} %refs_0_.1, bf16[2,128,1280]{2,1,0:T(8,128)(2,1)} %refs_1_.1, bf16[2,128,1280]{2,1,0:T(8,128)(2,1)} %refs_2_.1), custom_call_target="tpu_custom_call" | custom-call | tf_op jit(solution)/shard_map/pallas_call | solution.py:277
  18.0 0.9 %shard_map.38 = bf16[2,128,1280]{2,1,0:T(8,128)(2,1)} custom-call(f32[2,20,128]{2,1,0:T(8,128)S(1)} %get-tuple-element.9.enter, f32[2,128,1280]{2,1,0:T(8,128)S(1)} %get-tuple-element.10.keep_fore, f32[2,128,1280]{2,1,0:T(8,128)S(1)} %get-tuple-element.11.keep_back, f32[2,128,1280]{2,1,0:T(8,128)S(1)} %get-tuple-element.12.local), custom_call_target="tpu_custom_call" | custom-call | tf_op jit(solution)/shard_map/pallas_call | solution.py:293

commit v6 on v5

--- a/solution.py
+++ b/solution.py
@@ -10,37 +10,38 @@
 
 SPAN = ("slab", "place")
 MESH = pl.DeviceIdType.MESH
-TILE, LANES, GROUP, CHUNK = 256, 128, 640, 2
+TILE, LANES, CHUNK = 256, 128, 2
 FORE, DECAY, BACK = 0, 1, 2
 
 AROUND = ((2, 1), (1, 1), (3, 1), (2, 0), (0, 1), (1, 0), (3, 0))
 
 
 def kernel(
-    length, leak_hbm, signal_hbm, gate_hbm, enter, keep_fore, keep_back, local,
-    leak, signal, gate, since_ref, ahead_of, lower, upper, near, far,
+    length, leak_hbm, signal_hbm, gate_hbm, enter, keep_back, local,
+    leak, signal, gate, since_ref, keep_fore, ahead_of, lower, upper, near, far,
     load_sem, near_sem, far_sem, later_sem,
 ):
     batch, steps, channels = leak.shape
     groups = channels // LANES
     z, me = lax.axis_index("slab"), lax.axis_index("place")
-    parts = [
-        (b, slice(None), slice(c, c + GROUP)) for b in range(batch) for c in range(0, channels, GROUP)
-    ]
-
-    def load(which, k):
-        hbm, vmem = ((leak_hbm, leak), (signal_hbm, signal))[which]
-        return pltpu.make_async_copy(hbm.at[parts[k]], vmem.at[parts[k]], load_sem.at[which, k])
-
-    for k in range(len(parts)):
-        for which in range(2):
-            load(which, k).start()
-    gate_load = pltpu.make_async_copy(gate_hbm, gate, load_sem.at[0, 0])
+    parts = [(0, slice(None), slice(0, channels // 2)), (0, slice(None), slice(channels // 2, channels))]
+    parts += [(b, slice(None), slice(0, channels)) for b in range(1, batch)]
+
+    for k, part in enumerate(parts):
+        pltpu.make_async_copy(leak_hbm.at[part], leak.at[part], load_sem.at[k]).start()
+        pltpu.make_async_copy(signal_hbm.at[part], signal.at[part], load_sem.at[k]).start()
+
+    def wait_load(k):
+        halves = (parts[k][2].stop - parts[k][2].start) * 2 // channels
+        both = leak.at[pl.ds(0, halves), pl.ds(0, steps * 3 // 4)]
+        pltpu.make_async_copy(both, both, load_sem.at[k]).wait()
+
+    gate_load = pltpu.make_async_copy(gate_hbm, gate, load_sem.at[0])
     barrier = pltpu.get_barrier_semaphore()
-    for d in range(1, 8):
-        pl.semaphore_signal(
-            barrier, inc=1, device_id={"place": lax.rem(me + d, 8)}, device_id_type=MESH
-        )
+    y, x = lax.div(me, 2), lax.rem(me, 2)
+    others = [lax.rem(y + dy, 4) * 2 + lax.rem(x + dx, 2) for dy, dx in AROUND]
+    for i in others:
+        pl.semaphore_signal(barrier, inc=1, device_id={"place": i}, device_id_type=MESH)
     for i in range(1, 4):
 
         @pl.when(i > z)
@@ -68,9 +69,8 @@
 
     def summarize(k):
         b, _, columns = parts[k]
-        for h in range(GROUP // LANES):
-            at = k * (GROUP // LANES) + h
-            start = columns.start + h * LANES
+        for start in range(columns.start, columns.stop, LANES):
+            at = b * groups + start // LANES
             lanes = slice(start, start + LANES)
             back = jnp.zeros((8, LANES), jnp.float32)
             for r in range(0, steps, 16):
@@ -82,8 +82,7 @@
             near[me, BACK, at : at + 1] = jnp.sum(back, 0, keepdims=True) * scale
 
     for k in range(len(parts)):
-        load(0, k).wait()
-        load(1, k).wait()
+        wait_load(k)
         add_up(k)
         if k:
             summarize(k - 1)
@@ -114,9 +113,6 @@
         )
 
     first, second = pl.ds(DECAY, 2), pl.ds(FORE, 1)
-    y, x = lax.div(me, 2), lax.rem(me, 2)
-    others = [lax.rem(y + dy, 4) * 2 + lax.rem(x + dx, 2) for dy, dx in AROUND]
-
     def to_slab(planes, kind):
         for i in range(2):
             pl.when(i != me)(within(i, planes, kind).start)
@@ -157,12 +153,12 @@
     near[me, FORE] = near[me, FORE] * (own * scale)
     to_slab(second, 1)
 
-    def across(i, planes):
+    def across(i, kind):
         return pltpu.make_async_remote_copy(
-            src_ref=far.at[z, planes],
-            dst_ref=far.at[z, planes],
-            send_sem=far_sem.at[0],
-            recv_sem=far_sem.at[1],
+            src_ref=far.at[kind, z],
+            dst_ref=far.at[kind, z],
+            send_sem=far_sem.at[2],
+            recv_sem=far_sem.at[kind],
             device_id={"slab": i},
             device_id_type=MESH,
         )
@@ -175,10 +171,10 @@
     for s in reversed(range(8)):
         inside_back = jnp.where(me == s, state, inside_back)
         state = state * kept[s] + near[s, BACK]
-    far[z, BACK] = state
-    far[z, DECAY] = sum(decay[1:], decay[0])
+    far[0, z, 1] = state
+    far[0, z, 0] = far[1, z, 0] = sum(decay[1:], decay[0])
     for i in range(3):
-        pl.when(i < z)(across(i, pl.ds(DECAY, 2)).start)
+        pl.when(i < z)(across(i, 0).start)
     for i in range(3):
 
         @pl.when(i < z)
@@ -193,19 +189,19 @@
     for s in range(8):
         inside_fore = jnp.where(me == s, state, inside_fore)
         state = state * kept[s] + near[s, FORE]
-    far[z, FORE] = state
+    far[1, z, 1] = state
 
     @pl.when(z < 3)
     def _():
         pl.semaphore_wait(later_sem.at[0], 1)
-        across(lax.rem(z + 1, 4), pl.ds(FORE, 2)).start()
+        across(lax.rem(z + 1, 4), 1).start()
 
     @pl.when(z < 2)
     def _():
         pl.semaphore_wait(later_sem.at[1], 2 - z)
 
     for i in range(2, 4):
-        pl.when(i > z + 1)(across(i, pl.ds(FORE, 2)).start)
+        pl.when(i > z + 1)(across(i, 1).start)
 
     ahead = behind = zero
     for s in range(8):
@@ -215,30 +211,39 @@
     inside_back = inside_back * own
     all_within(slice(None), 0).wait_send()
 
-    three = far.at[pl.ds(0, 2)]
-    all_across = pltpu.make_async_remote_copy(
-        src_ref=three,
-        dst_ref=three,
-        send_sem=far_sem.at[0],
-        recv_sem=far_sem.at[1],
-        device_id={"slab": z},
-        device_id_type=MESH,
-    )
-    all_across.wait_recv()
-    kept = [jnp.exp2(-far[s, DECAY]) for s in range(4)]
+    def all_across(n, kind):
+        part = far.at[kind, pl.ds(0, n)]
+        return pltpu.make_async_remote_copy(
+            src_ref=part,
+            dst_ref=part,
+            send_sem=far_sem.at[2],
+            recv_sem=far_sem.at[kind],
+            device_id={"slab": z},
+            device_id_type=MESH,
+        )
+
+    for n in range(1, 4):
+        pl.when(z == n)(all_across(n, 1).wait_recv)
     state = zero
-    for s in range(4):
-        state = jnp.where(s < z, state * kept[s] + far[s, FORE], state)
+    for s in range(3):
+        state = jnp.where(s < z, state * jnp.exp2(-far[1, s, 0]) + far[1, s, 1], state)
     enter[0] = inside_fore + reach_fore * state
+    for b in range(batch):
+        for n in range(groups):
+            part = (b, slice(None), slice(n * LANES, (n + 1) * LANES))
+            at = b * groups + n
+            local[part] = local[part] + keep_fore[part] * enter[0, at : at + 1]
+
+    for n in range(1, 4):
+        pl.when(z == 3 - n)(all_across(n, 0).wait_recv)
     state = zero
-    for s in reversed(range(4)):
-        state = jnp.where(s > z, state * kept[s] + far[s, BACK], state)
+    for s in (3, 2, 1):
+        state = jnp.where(s > z, state * jnp.exp2(-far[0, s, 0]) + far[0, s, 1], state)
     enter[1] = inside_back + reach_back * state
-
-    all_across.wait_send()
-
-
-def finish(enter, keep_fore, keep_back, local, out_hbm, out, sem):
+    all_across(3, 0).wait_send()
+
+
+def finish(enter, keep_back, local, out_hbm, out, sem):
     batch, _, channels = out.shape
     groups = channels // LANES
 
@@ -249,8 +254,7 @@
     for at in range(batch * groups):
         b, n = divmod(at, groups)
         part = (b, slice(None), slice(n * LANES, (n + 1) * LANES))
-        fore, back = enter[0, at : at + 1], enter[1, at : at + 1]
-        gated = local[part] + (keep_fore[part] * fore + keep_back[part] * back)
+        gated = local[part] + keep_back[part] * enter[1, at : at + 1]
         out[part] = gated.astype(jnp.bfloat16)
         if n % CHUNK == CHUNK - 1:
             store(b, n + 1 - CHUNK, n + 1).start()
@@ -276,24 +280,24 @@
         vmem = pl.BlockSpec(memory_space=pltpu.VMEM)
         states = pl.pallas_call(
             lambda *refs: kernel(length, *refs),
-            out_shape=[entering, wide_out, wide_out, wide_out],
+            out_shape=[entering, wide_out, wide_out],
             in_specs=[pl.BlockSpec(memory_space=pl.ANY)] * 3,
-            out_specs=[vmem] * 4,
+            out_specs=[vmem] * 3,
             scratch_shapes=[
-                wide, narrow, narrow, wide, triangle, triangle, triangle,
+                wide, narrow, narrow, wide, wide, triangle, triangle, triangle,
                 pltpu.VMEM((8, 3, rows, LANES), jnp.float32),
-                pltpu.VMEM((4, 3, rows, LANES), jnp.float32),
-                dma((2, batch * channels // GROUP)), dma((3,)), dma((2,)),
+                pltpu.VMEM((2, 4, 2, rows, LANES), jnp.float32),
+                dma((batch + 1,)), dma((3,)), dma((3,)),
                 pltpu.SemaphoreType.REGULAR((2,)),
             ],
             compiler_params=pltpu.CompilerParams(
-                collective_id=0, has_side_effects=True, vmem_limit_bytes=62_600_000
+                collective_id=0, has_side_effects=True, vmem_limit_bytes=63_900_000
             ),
         )(leak_rate, signal_in, gate_in)
         return pl.pallas_call(
             finish,
             out_shape=jax.ShapeDtypeStruct(shape, jnp.bfloat16),
-            in_specs=[vmem] * 4,
+            in_specs=[vmem] * 3,
             out_specs=pl.BlockSpec(memory_space=pl.ANY),
             scratch_shapes=[narrow, dma],
             compiler_params=pltpu.CompilerParams(vmem_limit_bytes=32 << 20),

time: 19.1 us -> 19.2 us (level)
  the two profiles are of different devices: /device:TPU:2 before, /device:TPU:24 now
where the time goes in v6:
time: 19.2 us; the launch traced here: 19 us
  Pallas kernels  19 us (99%)
    pallas_call x1, Pallas kernels, body(): pl.pallas_call(lambda *refs: kernel(length, *refs), out_shape=[entering,...  18.2 us
    pallas_call x1, Pallas kernels, body(): pl.pallas_call(finish, out_shape=jax.ShapeDtypeStruct(shape, jnp.bfloat16...  0.85 us

profile of v6, /device:TPU:24, one launch (start us, length us, event | category | flops | bytes accessed | tf_op | source)
XLA Modules:
  0.0 19.0 jit_solution(17166194136839031299)
XLA Ops:
  0.0 18.2 %shard_map.37 = (f32[2,20,128]{2,1,0:T(8,128)S(1)}, f32[2,128,1280]{2,1,0:T(8,128)S(1)}, f32[2,128,1280]{2,1,0:T(8,128)S(1)}) custom-call(f32[2,128,1280]{2,1,0:T(8,128)} %refs_0_.1, bf16[2,128,1280]{2,1,0:T(8,128)(2,1)} %refs_1_.1, bf16[2,128,1280]{2,1,0:T(8,128)(2,1)} %refs_2_.1), custom_call_target="tpu_custom_call" | custom-call | tf_op jit(solution)/shard_map/pallas_call | solution.py:281
  18.2 0.8 %shard_map.38 = bf16[2,128,1280]{2,1,0:T(8,128)(2,1)} custom-call(f32[2,20,128]{2,1,0:T(8,128)S(1)} %get-tuple-element.8.enter, f32[2,128,1280]{2,1,0:T(8,128)S(1)} %get-tuple-element.9.keep_back, f32[2,128,1280]{2,1,0:T(8,128)S(1)} %get-tuple-element.10.local), custom_call_target="tpu_custom_call" | custom-call | tf_op jit(solution)/shard_map/pallas_call | solution.py:297
